TPU v7x, 256 devices: a 8x8x2 block of a 8x8x16 slice. The times are simulated.
256 devices in a mesh: groups: 2 (over z), seq: 128 (over x, y, core).
Axes of the slice: x: 8, y: 8, z: 2, core: 2. Of those that a mesh axis runs over, the one named last changes fastest.
The devices are a block of a 8x8x16 slice.
Arguments:
- queries: bfloat16 [16384, 4096], P(('groups', 'seq')), parts along dimension 0, may hold values from -8 to 8
- keys: bfloat16 [16384, 512], P(('groups', 'seq')), parts along dimension 0, may hold values from -8 to 8
- values: bfloat16 [16384, 512], P(('groups', 'seq')), parts along dimension 0, may hold values from -6 to 6
- block_pairs: int32 [256], P('groups'), parts along dimension 0, may hold values from 0 to 127, each once
- decode_slots: int32 [256], P('groups'), parts along dimension 0, may hold values from 0 to 127, each once
Outputs:
- attended: bfloat16 [16384, 4096], P(('groups', 'seq')), parts along dimension 0
- decode_cache: bfloat16 [256, 256, 2, 128], P(('groups', 'seq')), parts along dimension 0
There are 2 independent parts, one for each index of `groups`. A program takes and returns all parts, laid end to end along the dimension named above; each array names one. Nothing has to cross between parts.
Inputs may be any that keep to these rules, and one draw needn't show every extreme that they name: `block_pairs`: each of 0 to 127 once. `decode_slots`: each of 0 to 127 once.
All inputs are finite; a program needn't handle non-finite values.
Results may differ from a plain program's by a relative error of at most 0.012.
The roundings to bfloat16 on the way count: a program that leaves them out, or rounds other values in their place, can miss the bound.
Values may be sent and summed in bfloat16 or wider, within the bound.
A program may use at most 128 MiB of HBM per device.

v0:
```python
import math

import jax
import jax.numpy as jnp
from jax import lax
from jax.sharding import PartitionSpec as P

HD = 128
KVH = 4
GQ = 8
QH = 32


ROPE_BASE = 500000.0
NEGATIVE = -1e30


def side_by_side(arrays, axis, dim, along):
    ends, at = ([], 0)
    for a in arrays[:-1]:
        at += a.shape[along]
        ends.append(at)
    both = jnp.concatenate(arrays, axis=along)
    return tuple(jnp.split(lax.all_gather(both, axis, axis=dim, tiled=True), ends, axis=along))


def rotate_rows(vectors, positions):
    half_dim = vectors.shape[-1] // 2
    frequency = ROPE_BASE ** (-(jnp.arange(half_dim, dtype=jnp.float32) * 2.0) / vectors.shape[-1])
    angles = positions.astype(jnp.float32)[:, None] * frequency[None, :]
    cosine_part = jnp.cos(angles)[:, None, :]
    sine_part = jnp.sin(angles)[:, None, :]
    first_half = vectors[..., :half_dim]
    second_half = vectors[..., half_dim:]
    return jnp.concatenate(
        [
            first_half * cosine_part - second_half * sine_part,
            second_half * cosine_part + first_half * sine_part,
        ],
        axis=-1,
    )


def token_positions(block_pairs, tok_dev):
    devices = block_pairs.shape[0]
    half_tok = tok_dev // 2
    within = jnp.arange(tok_dev, dtype=jnp.int32)
    late_flag = (within >= half_tok).astype(jnp.int32)
    block_index = (
        block_pairs[:, None] * (1 - late_flag)[None, :]
        + (2 * devices - 1 - block_pairs[:, None]) * late_flag[None, :]
    )
    return (block_index * half_tok + (within % half_tok)[None, :]).reshape(-1)


def invert_table(lookup):
    entries = lookup.shape[0]
    labels = jnp.arange(entries, dtype=jnp.int32)
    matches = (lookup[None, :] == labels[:, None]).astype(jnp.int32)
    return jnp.sum(matches * labels[None, :], axis=1)


def empty_state(query_rows):
    lead_shape = query_rows.shape[:3]
    return (
        jnp.full(lead_shape, NEGATIVE, jnp.float32),
        jnp.zeros(lead_shape, jnp.float32),
        jnp.zeros(query_rows.shape, jnp.float32),
    )


def flash_update(state, query_rows, query_pos, key_rows, value_rows, key_pos):
    maxima, totals, mixture = state
    scores = jnp.einsum(
        "tkgd,ukd->tkgu", query_rows, key_rows, preferred_element_type=jnp.float32
    ) * (1.0 / math.sqrt(query_rows.shape[-1]))
    allowed = (key_pos[None, :] <= query_pos[:, None])[:, None, None, :]
    new_max = jnp.maximum(maxima, jnp.max(jnp.where(allowed, scores, NEGATIVE), axis=-1))
    weights = jnp.where(allowed, jnp.exp(scores - new_max[..., None]), 0.0)
    factor = jnp.exp(maxima - new_max)
    totals = factor * totals + jnp.sum(weights, axis=-1)
    mixture = factor[..., None] * mixture + jnp.einsum(
        "tkgu,ukd->tkgd",
        weights.astype(jnp.bfloat16),
        value_rows,
        preferred_element_type=jnp.float32,
    )
    return (new_max, totals, mixture)


def attend_tiles(state, query_rows, query_pos, key_rows, value_rows, key_pos):
    key_count = key_rows.shape[0]
    tile_rows = math.gcd(key_count, 512)
    last_query = jnp.max(query_pos)

    def advance(tile_index, running):
        tile_keys = lax.dynamic_slice_in_dim(key_rows, tile_index * tile_rows, tile_rows, 0)
        tile_values = lax.dynamic_slice_in_dim(value_rows, tile_index * tile_rows, tile_rows, 0)
        tile_pos = lax.dynamic_slice_in_dim(key_pos, tile_index * tile_rows, tile_rows, 0)

        def update(current):
            return flash_update(current, query_rows, query_pos, tile_keys, tile_values, tile_pos)

        def unchanged(current):
            return current

        return lax.cond(jnp.min(tile_pos) <= last_query, update, unchanged, running)

    return lax.fori_loop(0, key_count // tile_rows, advance, state)


def finish_state(state):
    return (state[2] / state[1][..., None]).astype(jnp.bfloat16)


def shards(queries, keys, values, block_pairs, decode_slots):
    tok_dev = queries.shape[0]
    half_tok = tok_dev // 2
    devices = lax.axis_size("seq")
    own_index = lax.axis_index("seq")
    stride = devices // KVH
    per_block = half_tok // stride
    cache_len = tok_dev * devices // stride
    everywhere = token_positions(block_pairs, tok_dev)
    local_pos = lax.dynamic_slice_in_dim(everywhere, own_index * tok_dev, tok_dev, 0)
    turned_queries = (
        rotate_rows(queries.astype(jnp.float32).reshape(tok_dev, QH, HD), local_pos)
        .astype(jnp.bfloat16)
        .reshape(tok_dev, KVH, GQ, HD)
    )
    turned_keys = rotate_rows(keys.astype(jnp.float32).reshape(tok_dev, KVH, HD), local_pos).astype(
        jnp.bfloat16
    )
    value_rows = values.reshape(tok_dev, KVH, HD)
    inverse = invert_table(block_pairs)
    early_queries = turned_queries[:half_tok]
    late_queries = turned_queries[half_tok:]
    early_pos = local_pos[:half_tok]
    late_pos = local_pos[half_tok:]
    start_carry = ((empty_state(early_queries), empty_state(late_queries)), ())
    pieces = side_by_side((turned_keys.reshape(tok_dev, KVH * HD), values), "seq", 0, 1)
    states = start_carry[0]
    piece_keys = pieces[0]
    key_count = piece_keys.shape[0]
    key_rows = piece_keys.reshape(key_count, KVH, HD)
    value_part = pieces[1].reshape(key_count, KVH, HD)
    early_state = attend_tiles(
        states[0], early_queries, early_pos, key_rows, value_part, everywhere
    )
    late_state = attend_tiles(states[1], late_queries, late_pos, key_rows, value_part, everywhere)
    states = (early_state, late_state)
    attended = jnp.concatenate([finish_state(states[0]), finish_state(states[1])], axis=0).reshape(
        tok_dev, QH * HD
    )
    stacked = jnp.stack([turned_keys, value_rows], axis=2).reshape(2, per_block, stride, KVH, 2, HD)
    by_slot = jnp.transpose(stacked, (3, 2, 0, 1, 4, 5)).reshape(devices, 2 * per_block, 2, HD)
    outgoing = jnp.take(by_slot, decode_slots, axis=0)
    incoming = lax.all_to_all(outgoing, "seq", split_axis=0, concat_axis=0, tiled=True).reshape(
        devices, 2, per_block, 2, HD
    )
    early_rows = jnp.take(incoming[:, 0], inverse, axis=0)
    late_rows = jnp.take(incoming[:, 1], inverse[::-1], axis=0)
    decode_rows = jnp.concatenate([early_rows, late_rows], axis=0).reshape(cache_len, 2, HD)
    return (attended, decode_rows[None])


def solution(mesh):
    placed = (
        P(("groups", "seq"), None),
        P(("groups", "seq"), None),
        P(("groups", "seq"), None),
        P("groups"),
        P("groups"),
    )
    return jax.shard_map(
        shards,
        mesh=mesh,
        in_specs=placed,
        out_specs=(P(("groups", "seq"), None), P(("groups", "seq"), None, None, None)),
        check_vma=False,
    )
```

profile of v0, /device:TPU:519, one launch (start us, length us, event | category | flops | bytes accessed | tf_op | source)
XLA Modules:
  0.0 397.1 jit_solution(11805993843882899275)
XLA Ops:
  14.9 27.3 %all-to-all-start = ((bf16[128,2,2,128]{3,2,1,0:T(2,128)(2,1)}), bf16[128,2,2,128]{3,2,1,0:T(2,128)(2,1)S(1)}, u32[]{:S(2)}, u32[]{:S(2)}) async-start(bf16[128,2,2,128]{3,2,1,0:T(2,128)(2,1)} %broadcast_select_fusion), calls=%async_computation | async-start | bytes 262144 | tf_op jit(solution)/shard_map/all_to_all | solution.py:158
  45.3 6.4 %all-to-all-done = bf16[128,2,2,128]{3,2,1,0:T(2,128)(2,1)S(1)} async-done(((bf16[128,2,2,128]{3,2,1,0:T(2,128)(2,1)}), bf16[128,2,2,128]{3,2,1,0:T(2,128)(2,1)S(1)}, u32[]{:S(2)}, u32[]{:S(2)}) %all-to-all-start) | async-done | bytes 131104 | tf_op jit(solution)/shard_map/all_to_all | solution.py:158
  54.5 73.3 %all-gather.2.cloned.1.call-done = bf16[8192,1024]{1,0:T(8,128)(2,1)} async-done(((bf16[64,1024]{1,0:T(8,128)(2,1)}), bf16[8192,1024]{1,0:T(8,128)(2,1)}) %all-gather.2.cloned.1.call-update) | async-done | bytes 16777232 | tf_op jit(solution)/shard_map/all_gather | solution.py:24
  127.8 11.3 %fusion.32 = (bf16[8192,512]{1,0:T(8,128)(2,1)}, bf16[8192,512]{1,0:T(8,128)(2,1)}) fusion(bf16[8192,1024]{1,0:T(8,128)(2,1)} %all-gather.2.cloned.1.call-done), kind=kLoop, calls=%fused_computation.90 | loop fusion | bytes 33554432 | tf_op jit(solution)/shard_map/split | solution.py:24
  139.2 11.3 %copy.120 = bf16[8192,512]{0,1:T(8,128)(2,1)} copy(bf16[8192,512]{1,0:T(8,128)(2,1)} %get-tuple-element.683) | data formatting | bytes 16777216
  150.5 11.9 %copy.102 = bf16[8192,4,128]{2,0,1:T(8,128)(2,1)} copy(bf16[8192,4,128]{0,2,1:T(8,128)(2,1)} %bitcast.96) | data formatting | bytes 16777216 | tf_op jit(solution)/shard_map/while | solution.py:109
  162.4 11.4 %copy.117 = bf16[8192,512]{0,1:T(8,128)(2,1)} copy(bf16[8192,512]{1,0:T(8,128)(2,1)} %get-tuple-element.684) | data formatting | bytes 16777216
  173.8 11.9 %copy.101 = bf16[8192,4,128]{2,0,1:T(8,128)(2,1)} copy(bf16[8192,4,128]{0,2,1:T(8,128)(2,1)} %bitcast.97) | data formatting | bytes 16777216 | tf_op jit(solution)/shard_map/while | solution.py:109
  185.8 101.3 %while.35 = (s32[]{:T(128)}, f32[32,4,8]{0,2,1:T(8,128)S(1)}, f32[32,4,8]{0,2,1:T(8,128)S(1)}, f32[32,4,8,128]{3,2,0,1:T(8,128)S(1)}, s32[8192]{0:T(1024)S(1)}, ...) while((s32[]{:T(128)}, f32[32,4,8]{0,2,1:T(8,128)S(1)}, ...), condition=%wide.region_15.16_spmd, body=%wide.region_9.15_spmd.sunk | while | flops 272910848 | bytes 8777161 | solution.py:109
  200.5 4.3 %conditional.5 = ((f32[32,4,8]{0,2,1:T(8,128)S(1)}, f32[32,4,8]{0,2,1:T(8,128)S(1)}, f32[32,4,8,128]{3,2,0,1:T(8,128)S(1)})) conditional(s32[]{:T(128)} %convert_element_type.79, (f32[32,4,8]{0,2,1:T(8,128)S(1)}, f32[32,4,8]{0,2,1:T(8,128)S(1)}, f32[32,4,8,128]{3,2,0,1:T(8,128)S(1)}) %tuple.120, (s32[512]{0:T(512)S(1)}, s32[32]{0:T(128)S(1)}, ...), branch_computations={%region_11.11_spmd, %region_12.14_spmd} | conditional | flops 272910336 | bytes 8772768 | solution.py:107
  206.8 4.3 %conditional.5 = ((f32[32,4,8]{0,2,1:T(8,128)S(1)}, f32[32,4,8]{0,2,1:T(8,128)S(1)}, f32[32,4,8,128]{3,2,0,1:T(8,128)S(1)})) conditional(s32[]{:T(128)} %convert_element_type.79, (f32[32,4,8]{0,2,1:T(8,128)S(1)}, f32[32,4,8]{0,2,1:T(8,128)S(1)}, f32[32,4,8,128]{3,2,0,1:T(8,128)S(1)}) %tuple.120, (s32[512]{0:T(512)S(1)}, s32[32]{0:T(128)S(1)}, ...), branch_computations={%region_11.11_spmd, %region_12.14_spmd} | conditional | flops 272910336 | bytes 8772768 | solution.py:107
  213.1 4.3 %conditional.5 = ((f32[32,4,8]{0,2,1:T(8,128)S(1)}, f32[32,4,8]{0,2,1:T(8,128)S(1)}, f32[32,4,8,128]{3,2,0,1:T(8,128)S(1)})) conditional(s32[]{:T(128)} %convert_element_type.79, (f32[32,4,8]{0,2,1:T(8,128)S(1)}, f32[32,4,8]{0,2,1:T(8,128)S(1)}, f32[32,4,8,128]{3,2,0,1:T(8,128)S(1)}) %tuple.120, (s32[512]{0:T(512)S(1)}, s32[32]{0:T(128)S(1)}, ...), branch_computations={%region_11.11_spmd, %region_12.14_spmd} | conditional | flops 272910336 | bytes 8772768 | solution.py:107
  225.8 4.3 %conditional.5 = ((f32[32,4,8]{0,2,1:T(8,128)S(1)}, f32[32,4,8]{0,2,1:T(8,128)S(1)}, f32[32,4,8,128]{3,2,0,1:T(8,128)S(1)})) conditional(s32[]{:T(128)} %convert_element_type.79, (f32[32,4,8]{0,2,1:T(8,128)S(1)}, f32[32,4,8]{0,2,1:T(8,128)S(1)}, f32[32,4,8,128]{3,2,0,1:T(8,128)S(1)}) %tuple.120, (s32[512]{0:T(512)S(1)}, s32[32]{0:T(128)S(1)}, ...), branch_computations={%region_11.11_spmd, %region_12.14_spmd} | conditional | flops 272910336 | bytes 8772768 | solution.py:107
  232.1 4.3 %conditional.5 = ((f32[32,4,8]{0,2,1:T(8,128)S(1)}, f32[32,4,8]{0,2,1:T(8,128)S(1)}, f32[32,4,8,128]{3,2,0,1:T(8,128)S(1)})) conditional(s32[]{:T(128)} %convert_element_type.79, (f32[32,4,8]{0,2,1:T(8,128)S(1)}, f32[32,4,8]{0,2,1:T(8,128)S(1)}, f32[32,4,8,128]{3,2,0,1:T(8,128)S(1)}) %tuple.120, (s32[512]{0:T(512)S(1)}, s32[32]{0:T(128)S(1)}, ...), branch_computations={%region_11.11_spmd, %region_12.14_spmd} | conditional | flops 272910336 | bytes 8772768 | solution.py:107
  244.8 4.3 %conditional.5 = ((f32[32,4,8]{0,2,1:T(8,128)S(1)}, f32[32,4,8]{0,2,1:T(8,128)S(1)}, f32[32,4,8,128]{3,2,0,1:T(8,128)S(1)})) conditional(s32[]{:T(128)} %convert_element_type.79, (f32[32,4,8]{0,2,1:T(8,128)S(1)}, f32[32,4,8]{0,2,1:T(8,128)S(1)}, f32[32,4,8,128]{3,2,0,1:T(8,128)S(1)}) %tuple.120, (s32[512]{0:T(512)S(1)}, s32[32]{0:T(128)S(1)}, ...), branch_computations={%region_11.11_spmd, %region_12.14_spmd} | conditional | flops 272910336 | bytes 8772768 | solution.py:107
  251.1 4.3 %conditional.5 = ((f32[32,4,8]{0,2,1:T(8,128)S(1)}, f32[32,4,8]{0,2,1:T(8,128)S(1)}, f32[32,4,8,128]{3,2,0,1:T(8,128)S(1)})) conditional(s32[]{:T(128)} %convert_element_type.79, (f32[32,4,8]{0,2,1:T(8,128)S(1)}, f32[32,4,8]{0,2,1:T(8,128)S(1)}, f32[32,4,8,128]{3,2,0,1:T(8,128)S(1)}) %tuple.120, (s32[512]{0:T(512)S(1)}, s32[32]{0:T(128)S(1)}, ...), branch_computations={%region_11.11_spmd, %region_12.14_spmd} | conditional | flops 272910336 | bytes 8772768 | solution.py:107
  257.5 4.3 %conditional.5 = ((f32[32,4,8]{0,2,1:T(8,128)S(1)}, f32[32,4,8]{0,2,1:T(8,128)S(1)}, f32[32,4,8,128]{3,2,0,1:T(8,128)S(1)})) conditional(s32[]{:T(128)} %convert_element_type.79, (f32[32,4,8]{0,2,1:T(8,128)S(1)}, f32[32,4,8]{0,2,1:T(8,128)S(1)}, f32[32,4,8,128]{3,2,0,1:T(8,128)S(1)}) %tuple.120, (s32[512]{0:T(512)S(1)}, s32[32]{0:T(128)S(1)}, ...), branch_computations={%region_11.11_spmd, %region_12.14_spmd} | conditional | flops 272910336 | bytes 8772768 | solution.py:107
  270.1 4.3 %conditional.5 = ((f32[32,4,8]{0,2,1:T(8,128)S(1)}, f32[32,4,8]{0,2,1:T(8,128)S(1)}, f32[32,4,8,128]{3,2,0,1:T(8,128)S(1)})) conditional(s32[]{:T(128)} %convert_element_type.79, (f32[32,4,8]{0,2,1:T(8,128)S(1)}, f32[32,4,8]{0,2,1:T(8,128)S(1)}, f32[32,4,8,128]{3,2,0,1:T(8,128)S(1)}) %tuple.120, (s32[512]{0:T(512)S(1)}, s32[32]{0:T(128)S(1)}, ...), branch_computations={%region_11.11_spmd, %region_12.14_spmd} | conditional | flops 272910336 | bytes 8772768 | solution.py:107
  276.4 4.3 %conditional.5 = ((f32[32,4,8]{0,2,1:T(8,128)S(1)}, f32[32,4,8]{0,2,1:T(8,128)S(1)}, f32[32,4,8,128]{3,2,0,1:T(8,128)S(1)})) conditional(s32[]{:T(128)} %convert_element_type.79, (f32[32,4,8]{0,2,1:T(8,128)S(1)}, f32[32,4,8]{0,2,1:T(8,128)S(1)}, f32[32,4,8,128]{3,2,0,1:T(8,128)S(1)}) %tuple.120, (s32[512]{0:T(512)S(1)}, s32[32]{0:T(128)S(1)}, ...), branch_computations={%region_11.11_spmd, %region_12.14_spmd} | conditional | flops 272910336 | bytes 8772768 | solution.py:107
  287.1 101.3 %while.34 = (s32[]{:T(128)}, f32[32,4,8]{0,2,1:T(8,128)S(1)}, f32[32,4,8]{0,2,1:T(8,128)S(1)}, f32[32,4,8,128]{3,2,0,1:T(8,128)S(1)}, s32[8192]{0:T(1024)S(1)}, ...) while((s32[]{:T(128)}, f32[32,4,8]{0,2,1:T(8,128)S(1)}, ...), condition=%wide.region_7.8_spmd, body=%wide.region_1.7_spmd.sunk | while | flops 272910848 | bytes 8777161 | solution.py:109
  301.8 4.3 %conditional.4 = ((f32[32,4,8]{0,2,1:T(8,128)S(1)}, f32[32,4,8]{0,2,1:T(8,128)S(1)}, f32[32,4,8,128]{3,2,0,1:T(8,128)S(1)})) conditional(s32[]{:T(128)} %convert_element_type.78, (f32[32,4,8]{0,2,1:T(8,128)S(1)}, f32[32,4,8]{0,2,1:T(8,128)S(1)}, f32[32,4,8,128]{3,2,0,1:T(8,128)S(1)}) %tuple.116, (s32[512]{0:T(512)S(1)}, s32[32]{0:T(128)S(1)}, ...), branch_computations={%region_3.3_spmd, %region_4.0_spmd} | conditional | flops 272910336 | bytes 8772768 | solution.py:107
  308.2 4.3 %conditional.4 = ((f32[32,4,8]{0,2,1:T(8,128)S(1)}, f32[32,4,8]{0,2,1:T(8,128)S(1)}, f32[32,4,8,128]{3,2,0,1:T(8,128)S(1)})) conditional(s32[]{:T(128)} %convert_element_type.78, (f32[32,4,8]{0,2,1:T(8,128)S(1)}, f32[32,4,8]{0,2,1:T(8,128)S(1)}, f32[32,4,8,128]{3,2,0,1:T(8,128)S(1)}) %tuple.116, (s32[512]{0:T(512)S(1)}, s32[32]{0:T(128)S(1)}, ...), branch_computations={%region_3.3_spmd, %region_4.0_spmd} | conditional | flops 272910336 | bytes 8772768 | solution.py:107
  314.5 4.3 %conditional.4 = ((f32[32,4,8]{0,2,1:T(8,128)S(1)}, f32[32,4,8]{0,2,1:T(8,128)S(1)}, f32[32,4,8,128]{3,2,0,1:T(8,128)S(1)})) conditional(s32[]{:T(128)} %convert_element_type.78, (f32[32,4,8]{0,2,1:T(8,128)S(1)}, f32[32,4,8]{0,2,1:T(8,128)S(1)}, f32[32,4,8,128]{3,2,0,1:T(8,128)S(1)}) %tuple.116, (s32[512]{0:T(512)S(1)}, s32[32]{0:T(128)S(1)}, ...), branch_computations={%region_3.3_spmd, %region_4.0_spmd} | conditional | flops 272910336 | bytes 8772768 | solution.py:107
  320.8 4.3 %conditional.4 = ((f32[32,4,8]{0,2,1:T(8,128)S(1)}, f32[32,4,8]{0,2,1:T(8,128)S(1)}, f32[32,4,8,128]{3,2,0,1:T(8,128)S(1)})) conditional(s32[]{:T(128)} %convert_element_type.78, (f32[32,4,8]{0,2,1:T(8,128)S(1)}, f32[32,4,8]{0,2,1:T(8,128)S(1)}, f32[32,4,8,128]{3,2,0,1:T(8,128)S(1)}) %tuple.116, (s32[512]{0:T(512)S(1)}, s32[32]{0:T(128)S(1)}, ...), branch_computations={%region_3.3_spmd, %region_4.0_spmd} | conditional | flops 272910336 | bytes 8772768 | solution.py:107
  327.2 4.3 %conditional.4 = ((f32[32,4,8]{0,2,1:T(8,128)S(1)}, f32[32,4,8]{0,2,1:T(8,128)S(1)}, f32[32,4,8,128]{3,2,0,1:T(8,128)S(1)})) conditional(s32[]{:T(128)} %convert_element_type.78, (f32[32,4,8]{0,2,1:T(8,128)S(1)}, f32[32,4,8]{0,2,1:T(8,128)S(1)}, f32[32,4,8,128]{3,2,0,1:T(8,128)S(1)}) %tuple.116, (s32[512]{0:T(512)S(1)}, s32[32]{0:T(128)S(1)}, ...), branch_computations={%region_3.3_spmd, %region_4.0_spmd} | conditional | flops 272910336 | bytes 8772768 | solution.py:107
  333.5 4.3 %conditional.4 = ((f32[32,4,8]{0,2,1:T(8,128)S(1)}, f32[32,4,8]{0,2,1:T(8,128)S(1)}, f32[32,4,8,128]{3,2,0,1:T(8,128)S(1)})) conditional(s32[]{:T(128)} %convert_element_type.78, (f32[32,4,8]{0,2,1:T(8,128)S(1)}, f32[32,4,8]{0,2,1:T(8,128)S(1)}, f32[32,4,8,128]{3,2,0,1:T(8,128)S(1)}) %tuple.116, (s32[512]{0:T(512)S(1)}, s32[32]{0:T(128)S(1)}, ...), branch_computations={%region_3.3_spmd, %region_4.0_spmd} | conditional | flops 272910336 | bytes 8772768 | solution.py:107
  346.2 4.3 %conditional.4 = ((f32[32,4,8]{0,2,1:T(8,128)S(1)}, f32[32,4,8]{0,2,1:T(8,128)S(1)}, f32[32,4,8,128]{3,2,0,1:T(8,128)S(1)})) conditional(s32[]{:T(128)} %convert_element_type.78, (f32[32,4,8]{0,2,1:T(8,128)S(1)}, f32[32,4,8]{0,2,1:T(8,128)S(1)}, f32[32,4,8,128]{3,2,0,1:T(8,128)S(1)}) %tuple.116, (s32[512]{0:T(512)S(1)}, s32[32]{0:T(128)S(1)}, ...), branch_computations={%region_3.3_spmd, %region_4.0_spmd} | conditional | flops 272910336 | bytes 8772768 | solution.py:107
  352.5 4.3 %conditional.4 = ((f32[32,4,8]{0,2,1:T(8,128)S(1)}, f32[32,4,8]{0,2,1:T(8,128)S(1)}, f32[32,4,8,128]{3,2,0,1:T(8,128)S(1)})) conditional(s32[]{:T(128)} %convert_element_type.78, (f32[32,4,8]{0,2,1:T(8,128)S(1)}, f32[32,4,8]{0,2,1:T(8,128)S(1)}, f32[32,4,8,128]{3,2,0,1:T(8,128)S(1)}) %tuple.116, (s32[512]{0:T(512)S(1)}, s32[32]{0:T(128)S(1)}, ...), branch_computations={%region_3.3_spmd, %region_4.0_spmd} | conditional | flops 272910336 | bytes 8772768 | solution.py:107
  365.2 4.3 %conditional.4 = ((f32[32,4,8]{0,2,1:T(8,128)S(1)}, f32[32,4,8]{0,2,1:T(8,128)S(1)}, f32[32,4,8,128]{3,2,0,1:T(8,128)S(1)})) conditional(s32[]{:T(128)} %convert_element_type.78, (f32[32,4,8]{0,2,1:T(8,128)S(1)}, f32[32,4,8]{0,2,1:T(8,128)S(1)}, f32[32,4,8,128]{3,2,0,1:T(8,128)S(1)}) %tuple.116, (s32[512]{0:T(512)S(1)}, s32[32]{0:T(128)S(1)}, ...), branch_computations={%region_3.3_spmd, %region_4.0_spmd} | conditional | flops 272910336 | bytes 8772768 | solution.py:107
  371.5 4.3 %conditional.4 = ((f32[32,4,8]{0,2,1:T(8,128)S(1)}, f32[32,4,8]{0,2,1:T(8,128)S(1)}, f32[32,4,8,128]{3,2,0,1:T(8,128)S(1)})) conditional(s32[]{:T(128)} %convert_element_type.78, (f32[32,4,8]{0,2,1:T(8,128)S(1)}, f32[32,4,8]{0,2,1:T(8,128)S(1)}, f32[32,4,8,128]{3,2,0,1:T(8,128)S(1)}) %tuple.116, (s32[512]{0:T(512)S(1)}, s32[32]{0:T(128)S(1)}, ...), branch_computations={%region_3.3_spmd, %region_4.0_spmd} | conditional | flops 272910336 | bytes 8772768 | solution.py:107
  377.8 4.3 %conditional.4 = ((f32[32,4,8]{0,2,1:T(8,128)S(1)}, f32[32,4,8]{0,2,1:T(8,128)S(1)}, f32[32,4,8,128]{3,2,0,1:T(8,128)S(1)})) conditional(s32[]{:T(128)} %convert_element_type.78, (f32[32,4,8]{0,2,1:T(8,128)S(1)}, f32[32,4,8]{0,2,1:T(8,128)S(1)}, f32[32,4,8,128]{3,2,0,1:T(8,128)S(1)}) %tuple.116, (s32[512]{0:T(512)S(1)}, s32[32]{0:T(128)S(1)}, ...), branch_computations={%region_3.3_spmd, %region_4.0_spmd} | conditional | flops 272910336 | bytes 8772768 | solution.py:107
  384.2 4.3 %conditional.4 = ((f32[32,4,8]{0,2,1:T(8,128)S(1)}, f32[32,4,8]{0,2,1:T(8,128)S(1)}, f32[32,4,8,128]{3,2,0,1:T(8,128)S(1)})) conditional(s32[]{:T(128)} %convert_element_type.78, (f32[32,4,8]{0,2,1:T(8,128)S(1)}, f32[32,4,8]{0,2,1:T(8,128)S(1)}, f32[32,4,8,128]{3,2,0,1:T(8,128)S(1)}) %tuple.116, (s32[512]{0:T(512)S(1)}, s32[32]{0:T(128)S(1)}, ...), branch_computations={%region_3.3_spmd, %region_4.0_spmd} | conditional | flops 272910336 | bytes 8772768 | solution.py:107
  (364 shorter events, 218.1 us)
Async XLA Ops:
  7.2 35.0 %copy-start.1 = (s32[128]{0:T(128)S(1)}, s32[128]{0:T(128)}, u32[]{:S(2)}) copy-start(s32[128]{0:T(128)} %param.18) | copy-start | bytes 1540
  7.2 5.9 %copy-start.2 = (s32[128]{0:T(128)S(1)}, s32[128]{0:T(128)}, u32[]{:S(2)}) copy-start(s32[128]{0:T(128)} %param.19) | copy-start | bytes 1540
  7.2 35.2 %copy-start = (bf16[64,4096]{1,0:T(8,128)(2,1)S(1)}, bf16[64,4096]{1,0:T(8,128)(2,1)}, u32[]{:S(2)}) copy-start(bf16[64,4096]{1,0:T(8,128)(2,1)} %param.15) | copy-start | bytes 1572868
  7.2 120.6 %all-gather.2.cloned.1.call-start = ((), (), s32[]{:S(2)}) async-start(), calls=%async_computation.1 | async-start | bytes 16908288 | tf_op jit(solution)/shard_map/all_gather | solution.py:24
  14.9 36.8 %all-to-all-start = ((bf16[128,2,2,128]{3,2,1,0:T(2,128)(2,1)}), bf16[128,2,2,128]{3,2,1,0:T(2,128)(2,1)S(1)}, u32[]{:S(2)}, u32[]{:S(2)}) async-start(bf16[128,2,2,128]{3,2,1,0:T(2,128)(2,1)} %broadcast_select_fusion), calls=%async_computation | async-start | bytes 262144 | tf_op jit(solution)/shard_map/all_to_all | solution.py:158
Sparse Core Ops, SparseCore 0:
  12.0 115.7 all-gather.1
where the time goes:
time: 403 us; the launch traced here: 397 us
  matrix products  109 us (27%)
  waiting for transfers between devices  79.7 us (20%)
  local copies, waits for them, and re-layouts  66.9 us (17%)
  other arithmetic  57.7 us (14%)
  loops' own time  42.4 us (11%)
  starting transfers between devices  27.3 us (7%)
  between operations  14.4 us (4%)
    all_gather x1, waiting for transfers between devices, side_by_side(): lax.all_gather(both, axis, axis=dim, tiled=True)  73.3 us
    dot_general x32, matrix products, flash_update(): jnp.einsum('tkgu,ukd->tkgd', weights.astype(jnp.bfloat16), value_rows, pr...  58.5 us
    dot_general x32, matrix products, flash_update(): jnp.einsum('tkgd,ukd->tkgu', query_rows, key_rows, preferred_element_type...  50.1 us
    another operation x2, loops' own time, attend_tiles(): return lax.fori_loop(0, key_count // tile_rows, advance, state)  40.7 us
    all_to_all x1, starting transfers between devices, shards(): lax.all_to_all(outgoing, 'seq', split_axis=0, concat_axis=0, tiled=True)  27.3 us
    reduce_min x32, other arithmetic, advance(): return lax.cond(jnp.min(tile_pos) <= last_query, update, unchanged, running)  25.2 us
    while x4, local copies, waits for them, and re-layouts, attend_tiles(): return lax.fori_loop(0, key_count // tile_rows, advance, state)  24 us
    unnamed x11, local copies, waits for them, and re-layouts  23.9 us
  transfers between devices with their start and end apart: 2, of which 2 were waited for; matrix products, arithmetic and copies ran while one was open for 2% of the time, Pallas kernels for 0%

commit v1 on v0

v1 whole, which is shorter than its diff:
```python
import functools
import math

import jax
import jax.numpy as jnp
import numpy as np
from jax import lax
from jax.experimental import pallas as pl
from jax.experimental.pallas import tpu as pltpu
from jax.sharding import PartitionSpec as P

HD = 128
KVH = 4
GQ = 8
QH = 32
ROPE_BASE = 500000.0
NEGATIVE = -1e30
MESH = pl.DeviceIdType.MESH
LOG_SCALE = math.log2(math.e) / math.sqrt(HD)
F32 = jnp.float32
BF16 = jnp.bfloat16


def place(side):
    me = lax.axis_index("seq")
    return me, me // (2 * side), (me // 2) % side, me % 2


def rotate(x, cosine, sine):
    return x * cosine + pltpu.roll(x, HD // 2, 1) * sine


def signs(h, far):
    return 1 if h in (0, far) else 2


def first_slot(h, side):
    return 0 if h == 0 else 2 * side * (2 * h - 1)


def prepare(side, pairs, slots, freq, keys, values, cosine, sine, packed, table):
    half = keys.shape[0] // 2
    devices = pairs.shape[0]
    far = side // 2
    me, x, y, core = place(side)
    own = pairs[me]
    row = lax.broadcasted_iota(jnp.int32, cosine.shape, 0)
    late = row >= half
    position = jnp.where(
        late, (2 * devices - 1 - own) * half + row - half, own * half + row
    )
    angle = position.astype(F32) * freq[...]
    lane = lax.broadcasted_iota(jnp.int32, cosine.shape, 1)
    cos_part = jnp.cos(angle)
    sin_part = jnp.sin(angle)
    sin_part = jnp.where(lane < HD // 2, -sin_part, sin_part)
    cosine[...] = cos_part
    sine[...] = sin_part
    for n in range(KVH):
        k = keys[:, n * HD : (n + 1) * HD].astype(F32)
        packed[n // 2, n % 2] = rotate(k, cos_part, sin_part).astype(BF16)
        packed[n // 2, 2 + n % 2] = values[:, n * HD : (n + 1) * HD]

    second = slots[me] // half >= KVH // 2

    def note(r, carry):
        dx = lax.rem(x - r // (2 * side) + side, side)
        dy = lax.rem(y - lax.rem(r // 2, side) + side, side)
        near = jnp.where(second, dy, dx)
        wide = jnp.where(second, dx, dy)
        i = jnp.where(
            near == 0,
            0,
            jnp.where(
                near == far,
                side - 1,
                jnp.where(near < far, 2 * near - 1, 2 * (side - near)),
            ),
        )
        back = (wide > far).astype(jnp.int32)
        h = jnp.where(wide > far, side - wide, wide)
        count = jnp.where(jnp.logical_or(h == 0, h == far), 1, 2)
        base = jnp.where(h == 0, 0, 2 * side * (2 * h - 1))
        slot = base + (lax.rem(r, 2) * count + back) * side + i
        table[pairs[r]] = slot
        return carry

    lax.fori_loop(0, devices, note, 0)


def attend(side, *refs):
    far = side // 2
    hops = far + 1
    pairs, slots, packed, queries, cosine, sine, mixture, weight, picked = refs[:9]
    rest = list(refs[9:])
    held = [[rest.pop(0) for _ in range(hops)] for _ in range(2)]
    got = [[rest.pop(0) for _ in range(hops)] for _ in range(2)]
    raw, turned, maxima, totals, found = rest[:5]
    query_sem, own_sem, near_sem, wide_sem, twin_out, twin_in = rest[5:]

    me, x, y, core = place(side)
    devices = pairs.shape[0]
    half = packed.shape[2] // 2
    rows = GQ * half
    step = 1 - 2 * core

    def chip(axis, shift):
        xs = lax.rem(x + shift + side, side) if axis == 0 else x
        ys = lax.rem(y + shift + side, side) if axis == 1 else y
        return {"seq": (xs * side + ys) * 2 + core}

    twin = {"seq": me + step}

    barrier = pltpu.get_barrier_semaphore()
    for target in (chip(0, 1), chip(0, -1), chip(1, 1), chip(1, -1), twin):
        pl.semaphore_signal(barrier, inc=1, device_id=target, device_id_type=MESH)
    load = pltpu.make_async_copy(queries, raw, query_sem)
    load.start()
    own_copies = [
        pltpu.make_async_copy(packed.at[p], held[p][0].at[core, 0], own_sem.at[p])
        for p in range(2)
    ]
    for copy in own_copies:
        copy.start()
    pl.semaphore_wait(barrier, 5)

    def remote(src, dst, send, recv, target):
        return pltpu.make_async_remote_copy(
            src_ref=src,
            dst_ref=dst,
            send_sem=send,
            recv_sem=recv,
            device_id=target,
            device_id_type=MESH,
        )

    def arrive(p, h, k):
        ref = held[p][h].at[core, k]
        remote(ref, ref, near_sem.at[p], got[p][h].at[k], twin).wait_recv()

    def near(p, src, k, target):
        remote(src, held[p][0].at[core, k], near_sem.at[p], got[p][0].at[k], target).start()

    def onward(p, h, src, k, target):
        remote(
            src, held[p][h + 1].at[core, k], wide_sem.at[p, h], got[p][h + 1].at[k], target
        ).start()

    def share(p, h, src, k):
        remote(src, held[p][h].at[core, k], twin_out.at[p, h], twin_in.at[p, h], twin).start()

    def first_tick(i):
        sources = []
        for p in range(2):
            if i == 0:
                src = packed.at[p]
                near(p, src, 1, chip(p, 1))
                near(p, src, 2, chip(p, -1))
            else:
                arrive(p, 0, i)
                src = held[p][0].at[core, i]
                k = (i + 1) // 2
                if k + 1 < far:
                    near(p, src, i + 2, chip(p, 1 if i % 2 else -1))
                elif k + 1 == far and i % 2 == 0:
                    near(p, held[p][0].at[core, i - 1 + core], side - 1, chip(p, step))
            sources.append(src)
        for p in range(2):
            onward(p, 0, sources[p], i, chip(1 - p, 1))
            onward(p, 0, sources[p], side + i, chip(1 - p, -1))
            share(p, 0, sources[p], i)

    def tick(h, i):
        for p in range(2):
            for s in range(signs(h, far)):
                k = s * side + i
                arrive(p, h, k)
                src = held[p][h].at[core, k]
                if h + 1 < far:
                    onward(p, h, src, k, chip(1 - p, 1 - 2 * s))
            if h + 1 == far:
                onward(p, h, held[p][h].at[core, core * side + i], i, chip(1 - p, step))
            for s in range(signs(h, far)):
                share(p, h, held[p][h].at[core, s * side + i], s * side + i)

    def turn(n):
        for g in range(GQ):
            q = n * GQ + g
            r = rotate(raw[:, q * HD : (q + 1) * HD].astype(F32), cosine[...], sine[...])
            r = r.astype(BF16)
            turned[n, g * half : (g + 1) * half] = r[:half]
            turned[n, rows + g * half : rows + (g + 1) * half] = r[half:]

    def scores(key_rows, query_rows):
        return lax.dot_general(
            key_rows, query_rows, (((1,), (1,)), ((), ())), preferred_element_type=F32
        )

    def mix(value_rows, weights):
        return lax.dot_general(
            value_rows, weights, (((0,), (0,)), ((), ())), preferred_element_type=F32
        )

    def begin(n):
        p, hh = n // 2, n % 2
        keys, values = packed[p, hh], packed[p, 2 + hh]
        u = lax.broadcasted_iota(jnp.int32, (half, rows), 0)
        t = lax.rem(lax.broadcasted_iota(jnp.int32, (half, rows), 1), half)
        for z in range(2):
            span = pl.ds(z * rows, rows)
            part = slice(z * half, (z + 1) * half)
            s = scores(keys[part], turned[n, span])
            s = jnp.where(u <= t, s, NEGATIVE)
            top = jnp.max(s, axis=0, keepdims=True)
            w = jnp.exp2((s - top) * LOG_SCALE)
            maxima[n, :, span] = top
            totals[n, :, span] = jnp.sum(w.reshape(half // 8, 8, rows), axis=0)
            mixture[n, :, span] = mix(values[part], w.astype(BF16))

    own = pairs[me]

    def block_of(p, h, cc, s, i):
        dx = 0 if i == 0 else far if i == side - 1 else (i + 1) // 2 if i % 2 else -(i // 2)
        shift = (1 - 2 * s) * h
        a = lax.rem((x if p == 0 else y) - dx + side, side)
        b = lax.rem((y if p == 0 else x) - shift + side, side)
        xs, ys = (a, b) if p == 0 else (b, a)
        return pairs[(xs * side + ys) * 2 + cc]

    def unit(p, h, cc, s, hh, early_bias, late_bias):
        n = 2 * p + hh
        ref = held[p][h]
        span = pl.ds(pl.multiple_of(s * side, side), side)
        count = side * half
        query_rows = turned[n]
        early = ref[cc, span, hh, :half].reshape(count, HD)
        late = ref[cc, span, hh, half:].reshape(count, HD)
        es = scores(early, query_rows)
        ls = scores(late, query_rows[rows:])
        e_parts = [
            es[i * half : (i + 1) * half, :rows] + early_bias[i] for i in range(side)
        ]
        f_part = es[:, rows:]
        l_parts = [ls[i * half : (i + 1) * half] + late_bias[i] for i in range(side)]
        e_top = functools.reduce(jnp.maximum, e_parts)
        l_top = functools.reduce(jnp.maximum, l_parts)
        f_top = jnp.max(f_part.reshape(side, half, rows), axis=0)
        top = jnp.concatenate([e_top, jnp.maximum(l_top, f_top)], axis=1)
        old = maxima[n]
        top = jnp.maximum(jnp.max(top, axis=0, keepdims=True), old)
        factor = jnp.exp2((old - top) * LOG_SCALE)
        maxima[n] = top
        level = top * LOG_SCALE
        e_level, l_level = level[:, :rows], level[:, rows:]
        ew = [jnp.exp2(v * LOG_SCALE - e_level) for v in e_parts]
        lw = [jnp.exp2(v * LOG_SCALE - l_level) for v in l_parts]
        fw = jnp.exp2(f_part * LOG_SCALE - l_level)
        e_sum = functools.reduce(jnp.add, ew).reshape(half // 8, 8, rows).sum(axis=0)
        l_sum = functools.reduce(jnp.add, lw).reshape(half // 8, 8, rows).sum(axis=0)
        f_sum = fw.reshape(count // 8, 8, rows).sum(axis=0)
        totals[n] = totals[n] * factor + jnp.concatenate([e_sum, l_sum + f_sum], axis=1)
        early_values = ref[cc, span, 2 + hh, :half].reshape(count, HD)
        late_values = ref[cc, span, 2 + hh, half:].reshape(count, HD)
        ew = jnp.concatenate([v.astype(BF16) for v in ew], axis=0)
        lw = jnp.concatenate([v.astype(BF16) for v in lw], axis=0)
        mixture[n, :, :rows] = mixture[n, :, :rows] * factor[:, :rows] + mix(early_values, ew)
        mixture[n, :, rows:] = (
            mixture[n, :, rows:] * factor[:, rows:]
            + mix(early_values, fw.astype(BF16))
            + mix(late_values, lw)
        )

    wanted = slots[me]
    wanted_head = wanted // half
    tile = lax.broadcasted_iota(jnp.int32, (16, HD), 0)
    picks = [
        [
            jnp.where(
                jnp.logical_and(
                    tile + part * 16 == lax.rem(wanted, half), lax.rem(wanted_head, 2) == hh
                ),
                1.0,
                0.0,
            ).astype(BF16)
            for part in range(half // 16)
        ]
        for hh in range(2)
    ]

    def collect(p, h, g, cc, s):
        span = pl.ds(pl.multiple_of(s * side, side), side)
        slot = pl.multiple_of(first_slot(h, side) + g * side, side)
        for z in range(2):
            for kind in range(2):
                terms = [
                    held[p][h][
                        cc, span, 2 * kind + hh, z * half + part * 16 : z * half + part * 16 + 16
                    ]
                    * picks[hh][part][None]
                    for hh in range(2)
                    for part in range(half // 16)
                ]
                row = functools.reduce(jnp.add, terms).astype(F32)
                found[p, 2 * z + kind, pl.ds(slot, side)] = jnp.sum(row, axis=1)

    def process(h, g):
        cc, s = g // signs(h, far), lax.rem(g, signs(h, far))
        for p in range(2):
            blocks = [block_of(p, h, cc, s, i) for i in range(side)]
            early_bias = [jnp.where(b < own, 0.0, NEGATIVE) for b in blocks]
            late_bias = [jnp.where(b > own, 0.0, NEGATIVE) for b in blocks]
            for hh in range(2):
                unit(p, h, cc, s, hh, early_bias, late_bias)
            collect(p, h, g, cc, s)

    def from_twin(h):
        for p in range(2):
            ref = held[p][h].at[1 - core]
            remote(ref, ref, twin_out.at[p, h], twin_in.at[p, h], twin).wait_recv()

    for i in range(side):
        first_tick(i)
        if i == 0:
            load.wait()
        if i < KVH:
            turn(i)
            begin(i)
    for copy in own_copies:
        copy.wait()

    for h in range(1, hops):
        groups = 2 * signs(h - 1, far)
        ticks = side // groups

        def ticks_of(g, h=h, ticks=ticks):
            for k in range(ticks):
                tick(h, g * ticks + k)

        ticks_of(0)
        from_twin(h - 1)

        def body(g, carry, h=h, groups=groups, ticks_of=ticks_of):
            process(h - 1, g)

            @pl.when(g + 1 < groups)
            def _():
                ticks_of(g + 1)

            return carry

        lax.fori_loop(0, groups, body, 0)

    from_twin(far)

    def last(g, carry):
        process(far, g)
        return carry

    lax.fori_loop(0, 2, last, 0)

    weight[...] = totals[...]
    second = wanted_head >= KVH // 2
    for kind in range(4):
        picked[kind] = jnp.where(second, found[1, kind], found[0, kind])

    for p in range(2):
        ref = held[p][0].at[core, pl.ds(1, side - 1)]
        remote(ref, ref, near_sem.at[p], got[p][0].at[0], twin).wait_send()
        for h in range(hops):
            if h < far:
                ref = held[p][h + 1].at[core]
                remote(ref, ref, wide_sem.at[p, h], got[p][0].at[0], twin).wait_send()
            ref = held[p][h].at[core]
            remote(ref, ref, twin_out.at[p, h], twin_in.at[p, h], twin).wait_send()


def finish(table, mixture, weight, picked, out, cache):
    half = out.shape[0] // 2
    rows = GQ * half
    devices = table.shape[0]
    for n in range(KVH):
        total = jnp.sum(weight[n], axis=0, keepdims=True)
        done = jnp.transpose(mixture[n] * (1.0 / total)).astype(BF16)
        for z in range(2):
            for g in range(GQ):
                q = n * GQ + g
                out[z * half : (z + 1) * half, q * HD : (q + 1) * HD] = done[
                    z * rows + g * half : z * rows + (g + 1) * half
                ]

    def emit(j, carry):
        slot = table[j]
        for z in range(2):
            pair = [picked[2 * z + kind, pl.ds(slot, 1)] for kind in range(2)]
            where = j if z == 0 else 2 * devices - 1 - j
            cache[where] = jnp.concatenate(pair, axis=0).astype(BF16)
        return carry

    lax.fori_loop(0, devices, emit, 0, unroll=4)


def shards(side, queries, keys, values, block_pairs, decode_slots):
    tok_dev = queries.shape[0]
    devices = block_pairs.shape[0]
    half = tok_dev // 2
    far = side // 2
    rows = GQ * half
    whole = 2 * rows
    exponent = -2.0 * (np.arange(HD) % (HD // 2)) / HD
    freq = jnp.asarray((ROPE_BASE**exponent).astype(np.float32)[None, :])
    vmem = pl.BlockSpec(memory_space=pltpu.VMEM)
    smem = pl.BlockSpec(memory_space=pltpu.SMEM)
    cosine, sine, packed, table = pl.pallas_call(
        functools.partial(prepare, side),
        out_shape=(
            jax.ShapeDtypeStruct((tok_dev, HD), F32),
            jax.ShapeDtypeStruct((tok_dev, HD), F32),
            jax.ShapeDtypeStruct((2, 4, tok_dev, HD), BF16),
            jax.ShapeDtypeStruct((devices,), jnp.int32),
        ),
        in_specs=[smem, smem, vmem, vmem, vmem],
        out_specs=(vmem, vmem, vmem, smem),
    )(block_pairs, decode_slots, freq, keys, values)
    held = [
        pltpu.VMEM((2, signs(h, far) * side, 4, tok_dev, HD), BF16) for h in range(far + 1)
    ]
    got = [pltpu.SemaphoreType.DMA((signs(h, far) * side,)) for h in range(far + 1)]
    mixture, weight, picked = pl.pallas_call(
        functools.partial(attend, side),
        out_shape=(
            jax.ShapeDtypeStruct((KVH, HD, whole), F32),
            jax.ShapeDtypeStruct((KVH, 8, whole), F32),
            jax.ShapeDtypeStruct((4, devices, HD), F32),
        ),
        in_specs=[smem, smem, vmem, pl.BlockSpec(memory_space=pl.ANY), vmem, vmem],
        out_specs=(vmem, vmem, vmem),
        scratch_shapes=[
            *held,
            *held,
            *got,
            *got,
            pltpu.VMEM((tok_dev, QH * HD), BF16),
            pltpu.VMEM((KVH, whole, HD), BF16),
            pltpu.VMEM((KVH, 1, whole), F32),
            pltpu.VMEM((KVH, 8, whole), F32),
            pltpu.VMEM((2, 4, devices, HD), F32),
            pltpu.SemaphoreType.DMA,
            pltpu.SemaphoreType.DMA((2,)),
            pltpu.SemaphoreType.DMA((2,)),
            pltpu.SemaphoreType.DMA((2, far)),
            pltpu.SemaphoreType.DMA((2, far + 1)),
            pltpu.SemaphoreType.DMA((2, far + 1)),
        ],
        compiler_params=pltpu.CompilerParams(
            collective_id=0, has_side_effects=True, vmem_limit_bytes=60 * 1024 * 1024
        ),
    )(block_pairs, decode_slots, packed, queries, cosine, sine)
    attended, cache = pl.pallas_call(
        finish,
        out_shape=(
            jax.ShapeDtypeStruct((tok_dev, QH * HD), BF16),
            jax.ShapeDtypeStruct((2 * devices, 2, HD), BF16),
        ),
        in_specs=[smem, vmem, vmem, vmem],
        out_specs=(vmem, vmem),
    )(table, mixture, weight, picked)
    return attended, cache[None]


def solution(mesh):
    side = math.isqrt(mesh.shape["seq"] // 2)
    placed = (
        P(("groups", "seq"), None),
        P(("groups", "seq"), None),
        P(("groups", "seq"), None),
        P("groups"),
        P("groups"),
    )
    return jax.shard_map(
        functools.partial(shards, side),
        mesh=mesh,
        in_specs=placed,
        out_specs=(P(("groups", "seq"), None), P(("groups", "seq"), None, None, None)),
        check_vma=False,
    )
```

time: 403 us -> 89.6 us (0.22)
  the two profiles are of different devices: /device:TPU:519 before, /device:TPU:513 now
where the time goes in v1:
time: 89.6 us; the launch traced here: 89.4 us
  Pallas kernels  88.7 us (99%)
    pallas_call x1, Pallas kernels, shards(): pl.pallas_call(functools.partial(attend, side), out_shape=(jax.ShapeDtype...  80.6 us
    pallas_call x1, Pallas kernels, shards(): pl.pallas_call(functools.partial(prepare, side), out_shape=(jax.ShapeDtyp...  5.33 us
    pallas_call x1, Pallas kernels, shards(): pl.pallas_call(finish, out_shape=(jax.ShapeDtypeStruct((tok_dev, QH * HD)...  2.86 us

profile of v1, /device:TPU:513, one launch (start us, length us, event | category | flops | bytes accessed | tf_op | source)
XLA Modules:
  0.0 89.4 jit_solution(9590838152806213906)
XLA Ops:
  0.6 5.3 %shard_map.77 = (f32[64,128]{1,0:T(8,128)}, f32[64,128]{1,0:T(8,128)}, bf16[2,4,64,128]{3,2,1,0:T(8,128)(2,1)}, s32[128]{0:T(128)}) custom-call(s32[128]{0:T(128)} %refs_0_.1, s32[128]{0:T(128)} %refs_1_.1, f32[1,128]{1,0:T(1,128)} %constant.2.clone.freq, bf16[64,512]{1,0:T(8,128)(2,1)} %keys.1, bf16[64,512]{1,0:T(8,128)(2,1)} %values.1), custom_call_target="tpu_custom_call" | custom-call | tf_op jit(solution)/shard_map/pallas_call | solution.py:413
  6.0 80.6 %shard_map.78 = (f32[4,128,512]{2,1,0:T(8,128)}, f32[4,8,512]{2,1,0:T(8,128)}, f32[4,128,128]{2,1,0:T(8,128)}) custom-call(s32[128]{0:T(128)} %refs_0_.1, s32[128]{0:T(128)} %refs_1_.1, bf16[2,4,64,128]{3,2,1,0:T(8,128)(2,1)} %get-tuple-element.12.refs_2_, bf16[64,4096]{1,0:T(8,128)(2,1)} %refs_3_.1, f32[64,128]{1,0:T(8,128)} %get-tuple-element.13.refs_4_, ...), custom_call_target="tpu_custom_call" | custom-call | tf_op jit(solution)/shard_map/pallas_call | solution.py:428
  86.5 2.9 %shard_map.79 = (bf16[64,4096]{1,0:T(8,128)(2,1)}, bf16[256,2,128]{2,1,0:T(2,128)(2,1)}) custom-call(s32[128]{0:T(128)} %get-tuple-element.11.table, f32[4,128,512]{2,1,0:T(8,128)} %get-tuple-element.15.mixture, f32[4,8,512]{2,1,0:T(8,128)} %get-tuple-element.16.weight, f32[4,128,128]{2,1,0:T(8,128)} %get-tuple-element.17.picked), custom_call_target="tpu_custom_call" | custom-call | tf_op jit(solution)/shard_map/pallas_call | solution.py:458

commit v2 on v1

--- a/solution.py
+++ b/solution.py
@@ -38,12 +38,10 @@
     return 0 if h == 0 else 2 * side * (2 * h - 1)
 
 
-def prepare(side, pairs, slots, freq, keys, values, cosine, sine, packed, table):
+def prepare(side, pairs, freq, keys, values, cosine, sine, packed):
     half = keys.shape[0] // 2
     devices = pairs.shape[0]
-    far = side // 2
-    me, x, y, core = place(side)
-    own = pairs[me]
+    own = pairs[place(side)[0]]
     row = lax.broadcasted_iota(jnp.int32, cosine.shape, 0)
     late = row >= half
     position = jnp.where(
@@ -60,32 +58,6 @@
         k = keys[:, n * HD : (n + 1) * HD].astype(F32)
         packed[n // 2, n % 2] = rotate(k, cos_part, sin_part).astype(BF16)
         packed[n // 2, 2 + n % 2] = values[:, n * HD : (n + 1) * HD]
-
-    second = slots[me] // half >= KVH // 2
-
-    def note(r, carry):
-        dx = lax.rem(x - r // (2 * side) + side, side)
-        dy = lax.rem(y - lax.rem(r // 2, side) + side, side)
-        near = jnp.where(second, dy, dx)
-        wide = jnp.where(second, dx, dy)
-        i = jnp.where(
-            near == 0,
-            0,
-            jnp.where(
-                near == far,
-                side - 1,
-                jnp.where(near < far, 2 * near - 1, 2 * (side - near)),
-            ),
-        )
-        back = (wide > far).astype(jnp.int32)
-        h = jnp.where(wide > far, side - wide, wide)
-        count = jnp.where(jnp.logical_or(h == 0, h == far), 1, 2)
-        base = jnp.where(h == 0, 0, 2 * side * (2 * h - 1))
-        slot = base + (lax.rem(r, 2) * count + back) * side + i
-        table[pairs[r]] = slot
-        return carry
-
-    lax.fori_loop(0, devices, note, 0)
 
 
 def attend(side, *refs):
@@ -188,8 +160,10 @@
             q = n * GQ + g
             r = rotate(raw[:, q * HD : (q + 1) * HD].astype(F32), cosine[...], sine[...])
             r = r.astype(BF16)
-            turned[n, g * half : (g + 1) * half] = r[:half]
-            turned[n, rows + g * half : rows + (g + 1) * half] = r[half:]
+            for z in range(2):
+                turned[n, g * half : (g + 1) * half, z * HD : (z + 1) * HD] = r[
+                    z * half : (z + 1) * half
+                ]
 
     def scores(key_rows, query_rows):
         return lax.dot_general(
@@ -207,15 +181,15 @@
         u = lax.broadcasted_iota(jnp.int32, (half, rows), 0)
         t = lax.rem(lax.broadcasted_iota(jnp.int32, (half, rows), 1), half)
         for z in range(2):
-            span = pl.ds(z * rows, rows)
             part = slice(z * half, (z + 1) * half)
-            s = scores(keys[part], turned[n, span])
+            deep = slice(z * HD, (z + 1) * HD)
+            s = scores(keys[part], turned[n, :, deep])
             s = jnp.where(u <= t, s, NEGATIVE)
             top = jnp.max(s, axis=0, keepdims=True)
             w = jnp.exp2((s - top) * LOG_SCALE)
-            maxima[n, :, span] = top
-            totals[n, :, span] = jnp.sum(w.reshape(half // 8, 8, rows), axis=0)
-            mixture[n, :, span] = mix(values[part], w.astype(BF16))
+            maxima[n, z] = top
+            totals[n, z] = jnp.sum(w.reshape(half // 8, 8, rows), axis=0)
+            mixture[n, deep] = mix(values[part], w.astype(BF16))
 
     own = pairs[me]
 
@@ -227,48 +201,64 @@
         xs, ys = (a, b) if p == 0 else (b, a)
         return pairs[(xs * side + ys) * 2 + cc]
 
-    def unit(p, h, cc, s, hh, early_bias, late_bias):
+    def both(ref, cc, span, k, flags):
+        pair = [
+            ref[cc, span, k, z * half : (z + 1) * half] * flags[z] for z in range(2)
+        ]
+        return jnp.concatenate(pair, axis=2).reshape(side * half, 2 * HD)
+
+    def fold(parts, op):
+        return functools.reduce(op, parts)
+
+    def tiles(v):
+        return [v[8 * i : 8 * i + 8] for i in range(v.shape[0] // 8)]
+
+    def unit_scores(p, h, cc, s, hh, flags):
+        span = pl.ds(pl.multiple_of(s * side, side), side)
+        ref = held[p][h]
+        query_rows = turned[2 * p + hh]
+        early = ref[cc, span, hh, :half].reshape(side * half, HD)
+        return (
+            scores(both(ref, cc, span, hh, flags), query_rows),
+            scores(early, query_rows[:, HD:]),
+        )
+
+    def unit_mix(p, h, cc, s, hh, flags, early, late, pair):
         n = 2 * p + hh
+        span = pl.ds(pl.multiple_of(s * side, side), side)
         ref = held[p][h]
-        span = pl.ds(pl.multiple_of(s * side, side), side)
-        count = side * half
-        query_rows = turned[n]
-        early = ref[cc, span, hh, :half].reshape(count, HD)
-        late = ref[cc, span, hh, half:].reshape(count, HD)
-        es = scores(early, query_rows)
-        ls = scores(late, query_rows[rows:])
-        e_parts = [
-            es[i * half : (i + 1) * half, :rows] + early_bias[i] for i in range(side)
+        mixed, full = pair
+        blocks = [mixed[i * half : (i + 1) * half] for i in range(side)]
+        tops = [fold(tiles(v), jnp.maximum) for v in blocks]
+        e_top = fold([jnp.where(early[i], tops[i], NEGATIVE) for i in range(side)], jnp.maximum)
+        l_top = fold([jnp.where(late[i], tops[i], NEGATIVE) for i in range(side)], jnp.maximum)
+        l_top = jnp.maximum(l_top, fold(tiles(full), jnp.maximum))
+        levels, factors = [], []
+        for z, top in enumerate((e_top, l_top)):
+            old = maxima[n, z]
+            new = jnp.maximum(jnp.max(top, axis=0, keepdims=True), old)
+            factors.append(jnp.exp2((old - new) * LOG_SCALE))
+            levels.append(new * LOG_SCALE)
+            maxima[n, z] = new
+        ws = [
+            jnp.exp2(
+                blocks[i] * LOG_SCALE
+                - jnp.where(early[i], levels[0], jnp.where(late[i], levels[1], -NEGATIVE))
+            )
+            for i in range(side)
         ]
-        f_part = es[:, rows:]
-        l_parts = [ls[i * half : (i + 1) * half] + late_bias[i] for i in range(side)]
-        e_top = functools.reduce(jnp.maximum, e_parts)
-        l_top = functools.reduce(jnp.maximum, l_parts)
-        f_top = jnp.max(f_part.reshape(side, half, rows), axis=0)
-        top = jnp.concatenate([e_top, jnp.maximum(l_top, f_top)], axis=1)
-        old = maxima[n]
-        top = jnp.maximum(jnp.max(top, axis=0, keepdims=True), old)
-        factor = jnp.exp2((old - top) * LOG_SCALE)
-        maxima[n] = top
-        level = top * LOG_SCALE
-        e_level, l_level = level[:, :rows], level[:, rows:]
-        ew = [jnp.exp2(v * LOG_SCALE - e_level) for v in e_parts]
-        lw = [jnp.exp2(v * LOG_SCALE - l_level) for v in l_parts]
-        fw = jnp.exp2(f_part * LOG_SCALE - l_level)
-        e_sum = functools.reduce(jnp.add, ew).reshape(half // 8, 8, rows).sum(axis=0)
-        l_sum = functools.reduce(jnp.add, lw).reshape(half // 8, 8, rows).sum(axis=0)
-        f_sum = fw.reshape(count // 8, 8, rows).sum(axis=0)
-        totals[n] = totals[n] * factor + jnp.concatenate([e_sum, l_sum + f_sum], axis=1)
-        early_values = ref[cc, span, 2 + hh, :half].reshape(count, HD)
-        late_values = ref[cc, span, 2 + hh, half:].reshape(count, HD)
-        ew = jnp.concatenate([v.astype(BF16) for v in ew], axis=0)
-        lw = jnp.concatenate([v.astype(BF16) for v in lw], axis=0)
-        mixture[n, :, :rows] = mixture[n, :, :rows] * factor[:, :rows] + mix(early_values, ew)
-        mixture[n, :, rows:] = (
-            mixture[n, :, rows:] * factor[:, rows:]
-            + mix(early_values, fw.astype(BF16))
-            + mix(late_values, lw)
-        )
+        fw = jnp.exp2(full * LOG_SCALE - levels[1])
+        sums = [fold(tiles(w), jnp.add) for w in ws]
+        e_sum = fold([jnp.where(early[i], sums[i], 0.0) for i in range(side)], jnp.add)
+        l_sum = fold([jnp.where(late[i], sums[i], 0.0) for i in range(side)], jnp.add)
+        totals[n, 0] = totals[n, 0] * factors[0] + e_sum
+        totals[n, 1] = totals[n, 1] * factors[1] + (l_sum + fold(tiles(fw), jnp.add))
+        w = jnp.concatenate([v.astype(BF16) for v in ws], axis=0)
+        o = mix(both(ref, cc, span, 2 + hh, flags), w)
+        values = ref[cc, span, 2 + hh, :half].reshape(side * half, HD)
+        f = mix(values, fw.astype(BF16))
+        mixture[n, :HD] = mixture[n, :HD] * factors[0] + o[:HD]
+        mixture[n, HD:] = mixture[n, HD:] * factors[1] + (o[HD:] + f)
 
     wanted = slots[me]
     wanted_head = wanted // half
@@ -305,12 +295,30 @@
 
     def process(h, g):
         cc, s = g // signs(h, far), lax.rem(g, signs(h, far))
+        todo = []
         for p in range(2):
             blocks = [block_of(p, h, cc, s, i) for i in range(side)]
-            early_bias = [jnp.where(b < own, 0.0, NEGATIVE) for b in blocks]
-            late_bias = [jnp.where(b > own, 0.0, NEGATIVE) for b in blocks]
+            early = [b < own for b in blocks]
+            late = [b > own for b in blocks]
+            flags = [
+                jnp.concatenate(
+                    [
+                        jnp.full((1, half, HD), jnp.where(f, 1.0, 0.0), F32).astype(BF16)
+                        for f in kind
+                    ],
+                    axis=0,
+                )
+                for kind in (early, late)
+            ]
             for hh in range(2):
-                unit(p, h, cc, s, hh, early_bias, late_bias)
+                todo.append((p, hh, flags, early, late))
+        pair = unit_scores(*todo[0][:1], h, cc, s, *todo[0][1:3])
+        for k, (p, hh, flags, early, late) in enumerate(todo):
+            held_pair = pair
+            if k + 1 < len(todo):
+                pair = unit_scores(todo[k + 1][0], h, cc, s, *todo[k + 1][1:3])
+            unit_mix(p, h, cc, s, hh, flags, early, late, held_pair)
+        for p in range(2):
             collect(p, h, g, cc, s)
 
     def from_twin(h):
@@ -374,29 +382,47 @@
             remote(ref, ref, twin_out.at[p, h], twin_in.at[p, h], twin).wait_send()
 
 
-def finish(table, mixture, weight, picked, out, cache):
+def finish(side, slots, pairs, mixture, weight, picked, out, cache):
     half = out.shape[0] // 2
-    rows = GQ * half
-    devices = table.shape[0]
+    devices = pairs.shape[1]
+    far = side // 2
+    me, x, y, core = place(side)
+    shape = (devices, devices)
+    row = lax.broadcasted_iota(jnp.int32, shape, 0)
+    r = lax.broadcasted_iota(jnp.int32, shape, 1)
+    dx = lax.rem(x - r // (2 * side) + side, side)
+    dy = lax.rem(y - lax.rem(r // 2, side) + side, side)
+    second = slots[me] // half >= KVH // 2
+    near = jnp.where(second, dy, dx)
+    wide = jnp.where(second, dx, dy)
+    i = jnp.where(near < far, 2 * near - 1, 2 * (side - near))
+    i = jnp.where(near == far, side - 1, jnp.where(near == 0, 0, i))
+    h = jnp.minimum(wide, side - wide)
+    group = lax.rem(r, 2) * jnp.where(jnp.logical_or(h == 0, h == far), 1, 2)
+    group = group + jnp.where(wide > far, 1, 0)
+    slot = jnp.where(h == 0, 0, 2 * side * (2 * h - 1)) + group * side + i
+    at_slot = jnp.where(slot == row, 1.0, 0.0).astype(BF16)
+    for z in range(2):
+        wanted = row if z == 0 else devices - 1 - row
+        at_block = jnp.where(pairs[...] == wanted, 1.0, 0.0).astype(BF16)
+        order = lax.dot_general(
+            at_block, at_slot, (((1,), (1,)), ((), ())), preferred_element_type=F32
+        ).astype(BF16)
+        for kind in range(2):
+            rows = picked[2 * z + kind].astype(BF16)
+            cache[z * devices : (z + 1) * devices, kind * HD : (kind + 1) * HD] = jnp.dot(
+                order, rows, preferred_element_type=F32
+            ).astype(BF16)
     for n in range(KVH):
-        total = jnp.sum(weight[n], axis=0, keepdims=True)
-        done = jnp.transpose(mixture[n] * (1.0 / total)).astype(BF16)
         for z in range(2):
+            total = jnp.sum(weight[n, z], axis=0, keepdims=True)
+            done = mixture[n, z * HD : (z + 1) * HD] * (1.0 / total)
+            done = jnp.transpose(done).astype(BF16)
             for g in range(GQ):
                 q = n * GQ + g
                 out[z * half : (z + 1) * half, q * HD : (q + 1) * HD] = done[
-                    z * rows + g * half : z * rows + (g + 1) * half
+                    g * half : (g + 1) * half
                 ]
-
-    def emit(j, carry):
-        slot = table[j]
-        for z in range(2):
-            pair = [picked[2 * z + kind, pl.ds(slot, 1)] for kind in range(2)]
-            where = j if z == 0 else 2 * devices - 1 - j
-            cache[where] = jnp.concatenate(pair, axis=0).astype(BF16)
-        return carry
-
-    lax.fori_loop(0, devices, emit, 0, unroll=4)
 
 
 def shards(side, queries, keys, values, block_pairs, decode_slots):
@@ -405,22 +431,20 @@
     half = tok_dev // 2
     far = side // 2
     rows = GQ * half
-    whole = 2 * rows
     exponent = -2.0 * (np.arange(HD) % (HD // 2)) / HD
     freq = jnp.asarray((ROPE_BASE**exponent).astype(np.float32)[None, :])
     vmem = pl.BlockSpec(memory_space=pltpu.VMEM)
     smem = pl.BlockSpec(memory_space=pltpu.SMEM)
-    cosine, sine, packed, table = pl.pallas_call(
+    cosine, sine, packed = pl.pallas_call(
         functools.partial(prepare, side),
         out_shape=(
             jax.ShapeDtypeStruct((tok_dev, HD), F32),
             jax.ShapeDtypeStruct((tok_dev, HD), F32),
             jax.ShapeDtypeStruct((2, 4, tok_dev, HD), BF16),
-            jax.ShapeDtypeStruct((devices,), jnp.int32),
         ),
-        in_specs=[smem, smem, vmem, vmem, vmem],
-        out_specs=(vmem, vmem, vmem, smem),
-    )(block_pairs, decode_slots, freq, keys, values)
+        in_specs=[smem, vmem, vmem, vmem],
+        out_specs=(vmem, vmem, vmem),
+    )(block_pairs, freq, keys, values)
     held = [
         pltpu.VMEM((2, signs(h, far) * side, 4, tok_dev, HD), BF16) for h in range(far + 1)
     ]
@@ -428,8 +452,8 @@
     mixture, weight, picked = pl.pallas_call(
         functools.partial(attend, side),
         out_shape=(
-            jax.ShapeDtypeStruct((KVH, HD, whole), F32),
-            jax.ShapeDtypeStruct((KVH, 8, whole), F32),
+            jax.ShapeDtypeStruct((KVH, 2 * HD, rows), F32),
+            jax.ShapeDtypeStruct((KVH, 2, 8, rows), F32),
             jax.ShapeDtypeStruct((4, devices, HD), F32),
         ),
         in_specs=[smem, smem, vmem, pl.BlockSpec(memory_space=pl.ANY), vmem, vmem],
@@ -440,9 +464,9 @@
             *got,
             *got,
             pltpu.VMEM((tok_dev, QH * HD), BF16),
-            pltpu.VMEM((KVH, whole, HD), BF16),
-            pltpu.VMEM((KVH, 1, whole), F32),
-            pltpu.VMEM((KVH, 8, whole), F32),
+            pltpu.VMEM((KVH, rows, 2 * HD), BF16),
+            pltpu.VMEM((KVH, 2, 1, rows), F32),
+            pltpu.VMEM((KVH, 2, 8, rows), F32),
             pltpu.VMEM((2, 4, devices, HD), F32),
             pltpu.SemaphoreType.DMA,
             pltpu.SemaphoreType.DMA((2,)),
@@ -456,15 +480,15 @@
         ),
     )(block_pairs, decode_slots, packed, queries, cosine, sine)
     attended, cache = pl.pallas_call(
-        finish,
+        functools.partial(finish, side),
         out_shape=(
             jax.ShapeDtypeStruct((tok_dev, QH * HD), BF16),
-            jax.ShapeDtypeStruct((2 * devices, 2, HD), BF16),
+            jax.ShapeDtypeStruct((2 * devices, 2 * HD), BF16),
         ),
-        in_specs=[smem, vmem, vmem, vmem],
+        in_specs=[smem, vmem, vmem, vmem, vmem],
         out_specs=(vmem, vmem),
-    )(table, mixture, weight, picked)
-    return attended, cache[None]
+    )(decode_slots, block_pairs[None, :], mixture, weight, picked)
+    return attended, cache.reshape(1, 2 * devices, 2, HD)
 
 
 def solution(mesh):

time: 89.6 us -> 85.2 us (0.951)
  Pallas kernels: 88.7 us -> 82.7 us
  local copies, waits for them, and re-layouts: 0 us -> 1.59 us
    pallas_call x1, Pallas kernels: 5.33 us -> 1.74 us  [shards(): pl.pallas_call(functools.partial(prepare, side), out_shape=(jax.ShapeDtyp...]
    pallas_call x1, Pallas kernels: 80.6 us -> 78.5 us  [shards(): pl.pallas_call(functools.partial(attend, side), out_shape=(jax.ShapeDtype...]
    reshape x0 -> x1, local copies, waits for them, and re-layouts: none -> 1.59 us  [shards(): return (attended, cache.reshape(1, 2 * devices, 2, HD))]
where the time goes in v2:
time: 85.2 us; the launch traced here: 84.9 us
  Pallas kernels  82.7 us (97%)
  local copies, waits for them, and re-layouts  1.59 us (2%)
    pallas_call x1, Pallas kernels, shards(): pl.pallas_call(functools.partial(attend, side), out_shape=(jax.ShapeDtype...  78.5 us
    pallas_call x1, Pallas kernels, shards(): pl.pallas_call(functools.partial(finish, side), out_shape=(jax.ShapeDtype...  2.48 us
    pallas_call x1, Pallas kernels, shards(): pl.pallas_call(functools.partial(prepare, side), out_shape=(jax.ShapeDtyp...  1.74 us

profile of v2, /device:TPU:513, one launch (start us, length us, event | category | flops | bytes accessed | tf_op | source)
XLA Modules:
  0.0 84.9 jit_solution(106928355781641762)
XLA Ops:
  0.6 1.7 %shard_map.77 = (f32[64,128]{1,0:T(8,128)}, f32[64,128]{1,0:T(8,128)}, bf16[2,4,64,128]{3,2,1,0:T(8,128)(2,1)}) custom-call(s32[128]{0:T(128)} %refs_0_.1, f32[1,128]{1,0:T(1,128)} %constant.2.clone.freq, bf16[64,512]{1,0:T(8,128)(2,1)} %keys.1, bf16[64,512]{1,0:T(8,128)(2,1)} %values.1), custom_call_target="tpu_custom_call" | custom-call | tf_op jit(solution)/shard_map/pallas_call | solution.py:438
  2.4 78.5 %shard_map.78 = (f32[4,256,256]{2,1,0:T(8,128)}, f32[4,2,8,256]{3,2,1,0:T(8,128)}, f32[4,128,128]{2,1,0:T(8,128)}) custom-call(s32[128]{0:T(128)} %refs_0_.1, s32[128]{0:T(128)} %slots.1, bf16[2,4,64,128]{3,2,1,0:T(8,128)(2,1)} %get-tuple-element.10.refs_2_, bf16[64,4096]{1,0:T(8,128)(2,1)} %refs_3_.1, f32[64,128]{1,0:T(8,128)} %get-tuple-element.11.refs_4_, ...), custom_call_target="tpu_custom_call" | custom-call | tf_op jit(solution)/shard_map/pallas_call | solution.py:452
  80.9 2.5 %shard_map.79 = (bf16[64,4096]{1,0:T(8,128)(2,1)}, bf16[256,256]{1,0:T(8,128)(2,1)}) custom-call(s32[128]{0:T(128)} %slots.1, s32[1,128]{1,0:T(1,128)} %bitcast.1, f32[4,256,256]{2,1,0:T(8,128)} %get-tuple-element.13.mixture, f32[4,2,8,256]{3,2,1,0:T(8,128)} %get-tuple-element.14.weight, f32[4,128,128]{2,1,0:T(8,128)} %get-tuple-element.15.picked), custom_call_target="tpu_custom_call" | custom-call | tf_op jit(solution)/shard_map/pallas_call | solution.py:482
  83.3 1.6 %reshape.7 = bf16[1,256,2,128]{3,2,1,0:T(2,128)(2,1)} reshape(bf16[256,256]{1,0:T(8,128)(2,1)} %get-tuple-element.17) | data formatting | bytes 262144 | tf_op jit(solution)/shard_map/reshape | solution.py:491
